TPU v7x, 32 devices: a whole 2x2x4 slice. The times are simulated.
32 devices in a mesh: section: 2 (over core), rows: 16 (over z, y, x).
Axes of the slice: x: 2, y: 2, z: 4, core: 2. Of those that a mesh axis runs over, the one named last changes fastest.
Arguments:
- table: float32 [16384, 64], P('rows', 'section'), may hold values from -6 to 6
- mask: int32 [16384], P('rows'), may hold values from 0 to 1, as said below
- weight: float32 [64, 1024], replicated, may hold values from -0.75 to 0.75
- bias: float32 [1024], replicated, may hold values from -3 to 3
Outputs:
- projected: bfloat16 [16384, 1024], P('rows', 'section')
Inputs may be any that keep to these rules, and one draw needn't show every extreme that they name: `mask`: the probability that a row survives is constant within one device's rows and drawn afresh for each device, from about 5 to 95 percent.
All inputs are finite; a program needn't handle non-finite values.
Results may differ from a plain program's by a relative error of at most 0.001.
Values sent between devices are 32-bit elements; how exact they have to be, the bound alone decides.
A program may use at most 64 MiB of HBM per device.

v0:
```python
import jax
import jax.numpy as jnp
from jax import lax
from jax.sharding import PartitionSpec as P


def passed_along(block, axis, distance):
    devices = range(lax.axis_size(axis))
    route = [(i - distance, i) for i in devices if i - distance in devices]
    return lax.ppermute(block, axis, route)


def from_partner(array, axis, bit):
    return lax.ppermute(array, axis, [(i, i ^ 1 << bit) for i in range(lax.axis_size(axis))])


def relocate(table, mask, rank, offset, myself, devices, edge_move, hop_move):
    height = table.shape[0]
    half = table.shape[1]
    local = jnp.arange(height, dtype=jnp.int32)
    target = offset + rank
    source = myself * height + local
    delta = source - target
    within = delta % height
    travel = delta // height
    slot = jnp.where(mask == 1, height + local - within, 2 * height)
    spread = jnp.zeros((2 * height, half), jnp.float32).at[slot].set(table, mode="drop")
    marker = jnp.zeros((2 * height,), jnp.int32).at[slot].set(travel + 1, mode="drop")
    arrived_rows, arrived_marks = edge_move((spread[:height], marker[:height]))
    packed = spread[height:] + arrived_rows
    marks = marker[height:] + arrived_marks
    levels = (devices - 1).bit_length()
    for level in range(levels):
        moving = (marks > 0) & ((marks - 1) // (1 << level) % 2 == 1)
        leaving_rows = jnp.where(moving[:, None], packed, 0.0)
        leaving_marks = jnp.where(moving, marks, 0)
        came_rows, came_marks = hop_move((leaving_rows, leaving_marks), -(1 << level))
        packed = jnp.where(moving[:, None], 0.0, packed) + came_rows
        marks = jnp.where(moving, 0, marks) + came_marks
    return (packed, marks)


def prefix_of(every, myself, devices):
    prefix = jnp.cumsum(every) - every
    offset = jnp.sum(jnp.where(jnp.arange(devices, dtype=jnp.int32) == myself, prefix, 0))
    return (prefix, offset)


def per_device(table, mask, weight, bias):
    height = table.shape[0]
    devices = lax.axis_size("rows")
    myself = lax.axis_index("rows")
    core = lax.axis_index("section")
    count = jnp.sum(mask)
    local = jnp.arange(height, dtype=jnp.int32)
    rank = jnp.cumsum(mask) - mask
    every = lax.all_gather(count.reshape(1), "rows", axis=0, tiled=True)
    prefix, offset = prefix_of(every, myself, devices)

    def edge_counted(couple):
        return passed_along(couple, "rows", -1)

    def hop_counted(couple, stride):
        return passed_along(couple, "rows", stride)

    packed, marks = relocate(table, mask, rank, offset, myself, devices, edge_counted, hop_counted)
    total = lax.psum(count, "rows")
    filled = myself * height + local < total
    width = weight.shape[1] // lax.axis_size("section")
    own_bias = lax.dynamic_slice_in_dim(bias, core * width, width, 0)
    other = from_partner(packed, "section", 0)
    joined = jnp.where(
        core == 0, jnp.concatenate([packed, other], 1), jnp.concatenate([other, packed], 1)
    )
    own_weight = lax.dynamic_slice_in_dim(weight, core * width, width, 1)
    result = jnp.dot(
        joined, own_weight, precision=lax.Precision.HIGHEST, preferred_element_type=jnp.float32
    )
    result = result + own_bias
    return jnp.where(filled[:, None], result, 0.0).astype(jnp.bfloat16)


def solution(mesh):
    return jax.shard_map(
        per_device,
        mesh=mesh,
        in_specs=(P("rows", "section"), P("rows"), P(), P()),
        out_specs=P("rows", "section"),
        check_vma=False,
    )
```

profile of v0, /device:TPU:3, one launch (start us, length us, event | category | flops | bytes accessed | tf_op | source)
XLA Modules:
  0.0 120.9 jit_solution(6495535973120791333)
XLA Ops:
  0.0 0.0 copy-start
  0.0 1.4 %reduce_sum.18 = s32[]{:T(128)} reduce(s32[1024]{0:T(1024)} %param.5, s32[]{:T(128)} %constant.109.clone.1), dimensions={0}, to_apply=%region_0.0 | reduce | flops 1023 | bytes 4104 | tf_op jit(solution)/shard_map/reduce_sum | solution.py:54
  1.4 1.3 %dynamic-slice = u32[1]{0:T(128)} dynamic-slice(u32[32]{0:T(128)} %constant.124, u32[]{:T(128)S(6)} %add.130), dynamic_slice_sizes={1} | dynamic-slice | bytes 12
  2.7 1.4 %dynamic-update-slice = s32[16]{0:T(128)S(1)} dynamic-update-slice(s32[16]{0:T(128)S(1)} %broadcast.77, s32[1]{0:T(128)} %bitcast, u32[]{:T(128)} %bitcast.1) | dynamic-update-slice | bytes 12
  4.1 11.6 %all-reduce.1 = (s32[]{:T(128)}, s32[16]{0:T(128)S(1)}) all-reduce(s32[]{:T(128)} %reduce_sum.18, s32[16]{0:T(128)S(1)} %dynamic-update-slice), channel_id=1, replica_groups=mesh['section'=2,'rows'=16] {'rows'}, use_global_device_ids=true, to_apply=%region_1.0 | all-reduce | flops 17 | bytes 136 | tf_op jit(solution)/shard_map/psum | solution.py:67
  15.7 1.0 reduce-window.21
  16.7 0.1 slice.19
  16.8 0.1 slice_reduce_fusion
  16.9 0.1 copy.6
  17.0 0.1 reduce
  17.2 0.7 fusion.37
  17.9 1.5 %fusion.11 = (s32[1024]{0:T(1024)S(1)}, s32[1024]{0:T(1024)S(1)}) fusion(s32[1024]{0:T(1024)} %param.5, s32[8,128]{1,0:T(8,128)S(1)} %reduce-window.21, s32[8]{0:T(128)S(1)} %slice_reduce_fusion, s32[]{:T(128)} %fusion.37, s32[]{:T(128)S(6)} %mul.8), kind=kLoop, calls=%fused_computation.54 | loop fusion | flops 32768 | bytes 16424 | tf_op jit(solution)/shard_map/add | solution.py:28
  19.3 4.3 %scatter_custom_fusion = s32[2048]{0:T(1024)S(1)} fusion(s32[1024]{0:T(1024)S(1)} %get-tuple-element.20, s32[1024]{0:T(1024)S(1)} %get-tuple-element.19, s32[]{:T(128)} %constant.109.clone.1), kind=kCustom, calls=%fused_computation.78 | custom fusion | bytes 8196 | tf_op jit(solution)/shard_map/scatter | solution.py:28
  23.7 2.2 %collective-permute-start = (s32[1024]{0:T(1024)S(1)}, s32[1024]{0:T(1024)S(1)}, u32[]{:S(2)}, u32[]{:S(2)}) collective-permute-start(s32[1024]{0:T(1024)S(1)} %slice.27), channel_id=1, source_target_pairs={{1,0},{2,1},{3,2},{4,3},{5,4},{6,5},{7,6},{8,7},{9,8},{10,9},{11,1... | collective-permute-start | bytes 12296 | tf_op jit(solution)/shard_map/ppermute | solution.py:10
  25.8 1.1 copy.7
  27.0 3.3 %scatter_custom_fusion.1 = f32[2048,32]{1,0:T(8,128)S(1)} fusion(s32[1024]{0:T(1024)S(1)} %get-tuple-element.20, f32[1024,32]{1,0:T(8,128)S(1)} %copy.7, f32[]{:T(128)} %constant.120.clone.1), kind=kCustom, calls=%fused_computation.14 | custom fusion | bytes 262148 | tf_op jit(solution)/shard_map/scatter | solution.py:27
  30.3 1.9 %collective-permute-start.4 = (f32[1024,32]{1,0:T(8,128)S(1)}, f32[1024,32]{1,0:T(8,128)S(1)}, u32[]{:S(2)}, u32[]{:S(2)}) collective-permute-start(f32[1024,32]{1,0:T(8,128)S(1)} %slice.29), channel_id=1, source_target_pairs={{1,0},{2,1},{3,2},{4,3},{5,4},{6,5},{7,6},{8,7},{9,8},{10,9},{11,1... | collective-permute-start | bytes 393224 | tf_op jit(solution)/shard_map/ppermute | solution.py:10
  32.3 0.0 collective-permute-done
  32.3 1.9 %collective-permute-start.1 = (s32[1024]{0:T(1024)S(1)}, s32[1024]{0:T(1024)S(1)}, u32[]{:S(2)}, u32[]{:S(2)}) collective-permute-start(s32[1024]{0:T(1024)S(1)} %get-tuple-element.17), channel_id=1, source_target_pairs={{1,0},{2,1},{3,2},{4,3},{5,4},{6,5},{7,6},{8,7},{9,8},{10,9},{11,1... | collective-permute-start | bytes 12296 | tf_op jit(solution)/shard_map/ppermute | solution.py:10
  34.2 7.7 %collective-permute-done.4 = f32[1024,32]{1,0:T(8,128)S(1)} collective-permute-done((f32[1024,32]{1,0:T(8,128)S(1)}, f32[1024,32]{1,0:T(8,128)S(1)}, u32[]{:S(2)}, u32[]{:S(2)}) %collective-permute-start.4) | collective-permute-done | bytes 131104 | tf_op jit(solution)/shard_map/ppermute | solution.py:10
  41.9 0.2 broadcast_select_fusion.3
  42.1 1.9 %collective-permute-start.5 = (f32[1024,32]{1,0:T(8,128)S(1)}, f32[1024,32]{1,0:T(8,128)S(1)}, u32[]{:S(2)}, u32[]{:S(2)}) collective-permute-start(f32[1024,32]{1,0:T(8,128)S(1)} %broadcast_select_fusion.3), channel_id=1, source_target_pairs={{1,0},{2,1},{3,2},{4,3},{5,4},{6,5},{7,6},{8,7},{9,8},{10,9},{11,1... | collective-permute-start | bytes 393224 | tf_op jit(solution)/shard_map/ppermute | solution.py:10
  44.0 0.0 collective-permute-done.1
  44.1 1.3 %collective-permute-start.2 = (s32[1024]{0:T(1024)S(1)}, s32[1024]{0:T(1024)S(1)}, u32[]{:S(2)}, u32[]{:S(2)}) collective-permute-start(s32[1024]{0:T(1024)S(1)} %get-tuple-element.14), channel_id=1, source_target_pairs={{2,0},{3,1},{4,2},{5,3},{6,4},{7,5},{8,6},{9,7},{10,8},{11,9},{12,... | collective-permute-start | bytes 12296 | tf_op jit(solution)/shard_map/ppermute | solution.py:10
  45.4 7.6 %collective-permute-done.5 = f32[1024,32]{1,0:T(8,128)S(1)} collective-permute-done((f32[1024,32]{1,0:T(8,128)S(1)}, f32[1024,32]{1,0:T(8,128)S(1)}, u32[]{:S(2)}, u32[]{:S(2)}) %collective-permute-start.5) | collective-permute-done | bytes 131104 | tf_op jit(solution)/shard_map/ppermute | solution.py:10
  53.0 0.3 broadcast_select_fusion.2
  53.3 1.3 %collective-permute-start.6 = (f32[1024,32]{1,0:T(8,128)S(1)}, f32[1024,32]{1,0:T(8,128)S(1)}, u32[]{:S(2)}, u32[]{:S(2)}) collective-permute-start(f32[1024,32]{1,0:T(8,128)S(1)} %get-tuple-element.12), channel_id=1, source_target_pairs={{2,0},{3,1},{4,2},{5,3},{6,4},{7,5},{8,6},{9,7},{10,8},{11,9},{12,... | collective-permute-start | bytes 393224 | tf_op jit(solution)/shard_map/ppermute | solution.py:10
  54.6 0.0 collective-permute-done.2
  54.7 1.3 %collective-permute-start.3 = (s32[1024]{0:T(1024)S(1)}, s32[1024]{0:T(1024)S(1)}, u32[]{:S(2)}, u32[]{:S(2)}) collective-permute-start(s32[1024]{0:T(1024)S(1)} %get-tuple-element.9), channel_id=1, source_target_pairs={{4,0},{5,1},{6,2},{7,3},{8,4},{9,5},{10,6},{11,7},{12,8},{13,9},{1... | collective-permute-start | bytes 12296 | tf_op jit(solution)/shard_map/ppermute | solution.py:10
  56.0 8.7 %collective-permute-done.6 = f32[1024,32]{1,0:T(8,128)S(1)} collective-permute-done((f32[1024,32]{1,0:T(8,128)S(1)}, f32[1024,32]{1,0:T(8,128)S(1)}, u32[]{:S(2)}, u32[]{:S(2)}) %collective-permute-start.6) | collective-permute-done | bytes 131104 | tf_op jit(solution)/shard_map/ppermute | solution.py:10
  64.7 0.3 broadcast_select_fusion.1
  65.0 1.3 %collective-permute-start.7 = (f32[1024,32]{1,0:T(8,128)S(1)}, f32[1024,32]{1,0:T(8,128)S(1)}, u32[]{:S(2)}, u32[]{:S(2)}) collective-permute-start(f32[1024,32]{1,0:T(8,128)S(1)} %broadcast_select_fusion.1), channel_id=1, source_target_pairs={{4,0},{5,1},{6,2},{7,3},{8,4},{9,5},{10,6},{11,7},{12,8},{13,9},{1... | collective-permute-start | bytes 393224 | tf_op jit(solution)/shard_map/ppermute | solution.py:10
  66.3 0.2 collective-permute-done.3
  66.5 13.9 %collective-permute-done.7 = f32[1024,32]{1,0:T(8,128)S(1)} collective-permute-done((f32[1024,32]{1,0:T(8,128)S(1)}, f32[1024,32]{1,0:T(8,128)S(1)}, u32[]{:S(2)}, u32[]{:S(2)}) %collective-permute-start.7) | collective-permute-done | bytes 131104 | tf_op jit(solution)/shard_map/ppermute | solution.py:10
  80.4 0.9 broadcast_select_fusion
  81.3 0.0 copy-start.1
  81.3 1.3 %collective-permute-start.8 = (f32[1024,32]{1,0:T(8,128)S(1)}, f32[1024,32]{1,0:T(8,128)S(1)}, u32[]{:S(2)}, u32[]{:S(2)}) collective-permute-start(f32[1024,32]{1,0:T(8,128)S(1)} %get-tuple-element.7), channel_id=1, source_target_pairs={{8,0},{9,1},{10,2},{11,3},{12,4},{13,5},{14,6},{15,7},{24,16},{25,... | collective-permute-start | bytes 393224 | tf_op jit(solution)/shard_map/ppermute | solution.py:10
  82.6 19.6 %collective-permute-done.8 = f32[1024,32]{1,0:T(8,128)S(1)} collective-permute-done((f32[1024,32]{1,0:T(8,128)S(1)}, f32[1024,32]{1,0:T(8,128)S(1)}, u32[]{:S(2)}, u32[]{:S(2)}) %collective-permute-start.8) | collective-permute-done | bytes 131104 | tf_op jit(solution)/shard_map/ppermute | solution.py:10
  102.2 0.2 select_add_fusion
  102.4 14.1 %collective-permute-start.9 = (f32[1024,32]{1,0:T(8,128)S(1)}, f32[1024,32]{1,0:T(8,128)S(1)}, u32[]{:S(2)}, u32[]{:S(2)}) collective-permute-start(f32[1024,32]{1,0:T(8,128)S(1)} %select_add_fusion), channel_id=1, source_target_pairs={{0,16},{16,0},{1,17},{17,1},{2,18},{18,2},{3,19},{19,3},{4,20},{20... | collective-permute-start | bytes 393224 | tf_op jit(solution)/shard_map/ppermute | solution.py:14
  116.5 0.0 copy-done.1
  116.5 0.1 dynamic_slice.7
  116.6 0.7 fusion.27
  117.2 0.8 collective-permute-done.9
  118.0 0.0 copy-done
  118.0 2.9 %select_convert_fusion = bf16[1024,512]{1,0:T(8,128)(2,1)} fusion(f32[512]{0:T(512)S(1)} %dynamic_slice.7, pred[1024]{0:T(1024)(128)(4,1)S(1)} %fusion.27, f32[1024,32]{1,0:T(8,128)S(1)} %collective-permute-done.9, f32[1024,32]{1,0:T(8,128)S(1)} %select_add_fusion, pred[]{:T(512)S(6)} %eq.30, f32[64,1024]{1,0:T(8,128)S(1)} %copy-done, s32[]{:T(128)S(6)} %select_n.139), kind=kOutput, calls=%fused_computation.2 | convolution fusion | flops 404422656 | bytes 2231301 | tf_op jit(solution)/shard_map/dot_general | solution.py:76
  (9 shorter events, 0.2 us)
Async XLA Ops:
  0.0 118.0 %copy-start = (f32[64,1024]{1,0:T(8,128)S(1)}, f32[64,1024]{1,0:T(8,128)}, u32[]{:S(2)}) copy-start(f32[64,1024]{1,0:T(8,128)} %param.6) | copy-start | bytes 786436
  23.7 8.6 %collective-permute-start = (s32[1024]{0:T(1024)S(1)}, s32[1024]{0:T(1024)S(1)}, u32[]{:S(2)}, u32[]{:S(2)}) collective-permute-start(s32[1024]{0:T(1024)S(1)} %slice.27), channel_id=1, source_target_pairs={{1,0},{2,1},{3,2},{4,3},{5,4},{6,5},{7,6},{8,7},{9,8},{10,9},{11,1... | collective-permute-start | bytes 12296 | tf_op jit(solution)/shard_map/ppermute | solution.py:10
  30.3 11.6 %collective-permute-start.4 = (f32[1024,32]{1,0:T(8,128)S(1)}, f32[1024,32]{1,0:T(8,128)S(1)}, u32[]{:S(2)}, u32[]{:S(2)}) collective-permute-start(f32[1024,32]{1,0:T(8,128)S(1)} %slice.29), channel_id=1, source_target_pairs={{1,0},{2,1},{3,2},{4,3},{5,4},{6,5},{7,6},{8,7},{9,8},{10,9},{11,1... | collective-permute-start | bytes 393224 | tf_op jit(solution)/shard_map/ppermute | solution.py:10
  32.3 11.7 %collective-permute-start.1 = (s32[1024]{0:T(1024)S(1)}, s32[1024]{0:T(1024)S(1)}, u32[]{:S(2)}, u32[]{:S(2)}) collective-permute-start(s32[1024]{0:T(1024)S(1)} %get-tuple-element.17), channel_id=1, source_target_pairs={{1,0},{2,1},{3,2},{4,3},{5,4},{6,5},{7,6},{8,7},{9,8},{10,9},{11,1... | collective-permute-start | bytes 12296 | tf_op jit(solution)/shard_map/ppermute | solution.py:10
  42.1 10.9 %collective-permute-start.5 = (f32[1024,32]{1,0:T(8,128)S(1)}, f32[1024,32]{1,0:T(8,128)S(1)}, u32[]{:S(2)}, u32[]{:S(2)}) collective-permute-start(f32[1024,32]{1,0:T(8,128)S(1)} %broadcast_select_fusion.3), channel_id=1, source_target_pairs={{1,0},{2,1},{3,2},{4,3},{5,4},{6,5},{7,6},{8,7},{9,8},{10,9},{11,1... | collective-permute-start | bytes 393224 | tf_op jit(solution)/shard_map/ppermute | solution.py:10
  44.1 10.5 %collective-permute-start.2 = (s32[1024]{0:T(1024)S(1)}, s32[1024]{0:T(1024)S(1)}, u32[]{:S(2)}, u32[]{:S(2)}) collective-permute-start(s32[1024]{0:T(1024)S(1)} %get-tuple-element.14), channel_id=1, source_target_pairs={{2,0},{3,1},{4,2},{5,3},{6,4},{7,5},{8,6},{9,7},{10,8},{11,9},{12,... | collective-permute-start | bytes 12296 | tf_op jit(solution)/shard_map/ppermute | solution.py:10
  53.3 11.3 %collective-permute-start.6 = (f32[1024,32]{1,0:T(8,128)S(1)}, f32[1024,32]{1,0:T(8,128)S(1)}, u32[]{:S(2)}, u32[]{:S(2)}) collective-permute-start(f32[1024,32]{1,0:T(8,128)S(1)} %get-tuple-element.12), channel_id=1, source_target_pairs={{2,0},{3,1},{4,2},{5,3},{6,4},{7,5},{8,6},{9,7},{10,8},{11,9},{12,... | collective-permute-start | bytes 393224 | tf_op jit(solution)/shard_map/ppermute | solution.py:10
  54.7 11.9 %collective-permute-start.3 = (s32[1024]{0:T(1024)S(1)}, s32[1024]{0:T(1024)S(1)}, u32[]{:S(2)}, u32[]{:S(2)}) collective-permute-start(s32[1024]{0:T(1024)S(1)} %get-tuple-element.9), channel_id=1, source_target_pairs={{4,0},{5,1},{6,2},{7,3},{8,4},{9,5},{10,6},{11,7},{12,8},{13,9},{1... | collective-permute-start | bytes 12296 | tf_op jit(solution)/shard_map/ppermute | solution.py:10
  65.0 15.4 %collective-permute-start.7 = (f32[1024,32]{1,0:T(8,128)S(1)}, f32[1024,32]{1,0:T(8,128)S(1)}, u32[]{:S(2)}, u32[]{:S(2)}) collective-permute-start(f32[1024,32]{1,0:T(8,128)S(1)} %broadcast_select_fusion.1), channel_id=1, source_target_pairs={{4,0},{5,1},{6,2},{7,3},{8,4},{9,5},{10,6},{11,7},{12,8},{13,9},{1... | collective-permute-start | bytes 393224 | tf_op jit(solution)/shard_map/ppermute | solution.py:10
  81.3 35.2 %copy-start.1 = (f32[1024]{0:T(1024)S(1)}, f32[1024]{0:T(1024)}, u32[]{:S(2)}) copy-start(f32[1024]{0:T(1024)} %param.7) | copy-start | bytes 12292
  81.3 20.9 %collective-permute-start.8 = (f32[1024,32]{1,0:T(8,128)S(1)}, f32[1024,32]{1,0:T(8,128)S(1)}, u32[]{:S(2)}, u32[]{:S(2)}) collective-permute-start(f32[1024,32]{1,0:T(8,128)S(1)} %get-tuple-element.7), channel_id=1, source_target_pairs={{8,0},{9,1},{10,2},{11,3},{12,4},{13,5},{14,6},{15,7},{24,16},{25,... | collective-permute-start | bytes 393224 | tf_op jit(solution)/shard_map/ppermute | solution.py:10
  102.4 15.6 %collective-permute-start.9 = (f32[1024,32]{1,0:T(8,128)S(1)}, f32[1024,32]{1,0:T(8,128)S(1)}, u32[]{:S(2)}, u32[]{:S(2)}) collective-permute-start(f32[1024,32]{1,0:T(8,128)S(1)} %select_add_fusion), channel_id=1, source_target_pairs={{0,16},{16,0},{1,17},{17,1},{2,18},{18,2},{3,19},{19,3},{4,20},{20... | collective-permute-start | bytes 393224 | tf_op jit(solution)/shard_map/ppermute | solution.py:14
where the time goes:
time: 121 us
  waiting for transfers between devices  58.5 us (48%)
  starting transfers between devices  28.5 us (24%)
  local copies, waits for them, and re-layouts  11.9 us (10%)
  blocking collectives  11.6 us (10%)
  other arithmetic  7.36 us (6%)
  matrix products  2.86 us (2%)
    ppermute x9, waiting for transfers between devices, passed_along(): return lax.ppermute(block, axis, route)  57.7 us
    ppermute x9, starting transfers between devices, passed_along(): return lax.ppermute(block, axis, route)  14.4 us
    ppermute x1, starting transfers between devices, from_partner(): lax.ppermute(array, axis, [(i, i ^ 1 << bit) for i in range(lax.axis_size...  14.1 us
    psum x1, blocking collectives, per_device(): total = lax.psum(count, 'rows')  11.6 us
    scatter x1, local copies, waits for them, and re-layouts, relocate(): jnp.zeros((2 * height,), jnp.int32).at[slot].set(travel + 1, mode='drop')  4.32 us
    unnamed x8, local copies, waits for them, and re-layouts  3.87 us
    scatter x1, local copies, waits for them, and re-layouts, relocate(): jnp.zeros((2 * height, half), jnp.float32).at[slot].set(table, mode='drop')  3.34 us
    dot_general x1, matrix products, per_device(): jnp.dot(joined, own_weight, precision=lax.Precision.HIGHEST, preferred_el...  2.86 us
  transfers between devices with their start and end apart: 10, of which 7 were waited for; matrix products, arithmetic and copies ran while one was open for 5% of the time, Pallas kernels for 0%

commit v1 on v0

v1 whole, which is shorter than its diff:
```python
import functools

import jax
import jax.numpy as jnp
from jax import lax
from jax.experimental import pallas as pl
from jax.experimental.pallas import tpu as pltpu
from jax.sharding import PartitionSpec as P

CHUNKS = 4
F32 = jnp.float32
BF16 = jnp.bfloat16
I32 = jnp.int32


def split(x, terms):
    parts = []
    for _ in range(terms):
        part = x.astype(BF16)
        parts.append(part)
        x = x - part.astype(F32)
    return parts


def kernel(
    n, table_ref, mask_ref, w_ref, bias_ref, out_ref,
    counts, prefix, hold, came, joined, wcat, send_sem, recv_sem, count_send, count_recv,
):
    height, half = table_ref.shape
    cols, width = w_ref.shape[0], out_ref.shape[1]
    lines = height // 128
    levels = (n - 1).bit_length()
    lanes = height // CHUNKS
    me = lax.axis_index("rows")
    core = lax.axis_index("section")

    barrier = pltpu.get_barrier_semaphore()

    def greet(step, carry):
        pl.semaphore_signal(barrier, inc=1, device_id={"rows": lax.rem(me + step, n)})
        return carry

    lax.fori_loop(1, n, greet, 0)
    pl.semaphore_signal(barrier, inc=1, device_id={"section": 1 - core})

    mask = mask_ref[...]
    ones = mask.astype(F32).astype(BF16)
    row = lax.broadcasted_iota(I32, (128, 128), 0)
    col = lax.broadcasted_iota(I32, (128, 128), 1)
    before = jnp.where(row < col, 1.0, 0.0).astype(BF16)
    inner = jnp.dot(ones, before, preferred_element_type=F32).astype(I32)
    sums = jnp.dot(ones, jnp.ones((128, 128), BF16), preferred_element_type=F32).astype(I32)
    running = jnp.zeros((1, 128), I32)
    starts = []
    for line in range(lines):
        starts.append(running)
        running = running + sums[line : line + 1]
    rank = inner + jnp.concatenate(starts, 0)
    counts[me] = running

    pl.semaphore_wait(barrier, n)

    def count_copy(step):
        peer = lax.rem(me + step, n)
        return pltpu.make_async_remote_copy(
            src_ref=counts.at[me], dst_ref=counts.at[me],
            send_sem=count_send.at[step], recv_sem=count_recv.at[step],
            device_id={"rows": peer},
        )

    def count_start(step, carry):
        count_copy(step).start()
        return carry

    def count_wait(step, carry):
        count_copy(step).wait()
        return carry

    lax.fori_loop(1, n, count_start, 0)

    w = w_ref[:, pl.ds(pl.multiple_of(core * width, 128), width)]
    bias = bias_ref[:, pl.ds(pl.multiple_of(core * width, 128), width)]
    w_hi, w_lo = split(w, 2)
    b_hi, b_mid, b_lo = [part.astype(F32) for part in split(bias, 3)]
    line = lax.broadcasted_iota(I32, (16, width), 0)
    extra = jnp.where(line == 0, b_hi, jnp.where(line == 1, b_mid, jnp.where(line == 2, b_lo, 0.0)))
    wcat[...] = jnp.concatenate([w_hi, w_lo, w_hi, extra.astype(BF16)], 0)
    turned = jnp.concatenate(split(table_ref[...].T, 3), 0)

    lax.fori_loop(1, n, count_wait, 0)
    total = jnp.zeros((1, 128), I32)
    for device in range(n):
        prefix[device] = total
        total = total + counts[device]
    prefix[n] = total

    slot = jnp.where(mask == 1, (rank + prefix[me]) & (height - 1), -1)

    def wide(x):
        return jnp.concatenate([x] * (lanes // 128), 1)

    def data_copy(level, chunk):
        at = (slice(None), pl.ds(chunk * lanes, lanes))
        return pltpu.make_async_remote_copy(
            src_ref=hold.at[(level,) + at], dst_ref=came.at[(level,) + at],
            send_sem=send_sem.at[level, chunk], recv_sem=recv_sem.at[level, chunk],
            device_id={"rows": me + (1 - 2 * (me // (1 << level) % 2)) * (1 << level)},
        )

    def join_copy(chunk):
        at = (core, slice(None), pl.ds(chunk * lanes, lanes))
        return pltpu.make_async_remote_copy(
            src_ref=joined.at[at], dst_ref=joined.at[at],
            send_sem=send_sem.at[levels, chunk], recv_sem=recv_sem.at[levels, chunk],
            device_id={"section": 1 - core},
        )

    for chunk in range(CHUNKS):
        here = chunk * lanes + lax.broadcasted_iota(I32, (lanes, 128), 0)
        hot = jnp.concatenate(
            [jnp.where(here == slot[b : b + 1], 1.0, 0.0).astype(BF16) for b in range(lines)], 1
        )
        folded = lax.dot_general(
            turned, hot, (((1,), (1,)), ((), ())), preferred_element_type=F32
        )
        hold[0, :, chunk * lanes : (chunk + 1) * lanes] = (
            folded[:half] + folded[half : 2 * half]
        ) + folded[2 * half :]
        data_copy(0, chunk).start()

    for level in range(levels):
        reach = 2 << level
        group = me // reach * reach
        bit = me // (1 << level) % 2
        low = wide(prefix[group])
        middle = wide(prefix[group + (1 << level)])
        for chunk in range(CHUNKS):
            at = slice(chunk * lanes, (chunk + 1) * lanes)
            data_copy(level, chunk).wait_recv()
            base = (me % reach) * height + chunk * lanes
            base = base + lax.broadcasted_iota(I32, (1, lanes), 1)
            place = low + ((base - low) & (reach * height - 1))
            upper = jnp.where(place >= middle, 1, 0)
            foreign = jnp.broadcast_to(upper, (half, lanes)) != bit
            block = jnp.where(foreign, came[level, :, at], hold[level, :, at])
            if level < levels - 1:
                hold[level + 1, :, at] = block
                data_copy(level + 1, chunk).start()
            else:
                joined[core, :, at] = block
                join_copy(chunk).start()

    ends = wide(total)
    for chunk in range(CHUNKS):
        at = slice(chunk * lanes, (chunk + 1) * lanes)
        join_copy(chunk).wait_recv()
        own = me * height + chunk * lanes + lax.broadcasted_iota(I32, (1, lanes), 1)
        filled = jnp.where(own < ends, 1.0, 0.0)
        rows = jnp.concatenate([joined[0, :, at], joined[1, :, at]], 0)
        rows = jnp.where(jnp.broadcast_to(filled, rows.shape) > 0.5, rows, 0.0)
        a_hi, a_lo = split(rows, 2)
        marks = jnp.broadcast_to(filled, (16, lanes)).astype(BF16)
        lhs = jnp.concatenate([a_hi, a_hi, a_lo, marks], 0)
        out_ref[at, :] = lax.dot_general(
            lhs, wcat[...], (((0,), (0,)), ((), ())), preferred_element_type=F32
        ).astype(BF16)

    for level in range(levels):
        for chunk in range(CHUNKS):
            data_copy(level, chunk).wait_send()
    for chunk in range(CHUNKS):
        join_copy(chunk).wait_send()


def solution(mesh):
    n, sections = mesh.shape["rows"], mesh.shape["section"]

    def step(table, mask, weight, bias):
        height, half = table.shape
        cols, features = weight.shape
        width = features // sections
        levels = (n - 1).bit_length()
        return pl.pallas_call(
            functools.partial(kernel, n),
            name="filter_project",
            out_shape=jax.ShapeDtypeStruct((height, width), BF16),
            in_specs=[pl.BlockSpec(memory_space=pltpu.VMEM)] * 4,
            out_specs=pl.BlockSpec(memory_space=pltpu.VMEM),
            scratch_shapes=[
                pltpu.VMEM((n, 1, 128), I32),
                pltpu.VMEM((n + 1, 1, 128), I32),
                pltpu.VMEM((levels, half, height), F32),
                pltpu.VMEM((levels, half, height), F32),
                pltpu.VMEM((sections, half, height), F32),
                pltpu.VMEM((3 * cols + 16, width), BF16),
                pltpu.SemaphoreType.DMA((levels + 1, CHUNKS)),
                pltpu.SemaphoreType.DMA((levels + 1, CHUNKS)),
                pltpu.SemaphoreType.DMA((n,)),
                pltpu.SemaphoreType.DMA((n,)),
            ],
            compiler_params=pltpu.CompilerParams(collective_id=0, has_side_effects=True),
        )(table, mask.reshape(height // 128, 128), weight, bias.reshape(1, features))

    return jax.shard_map(
        step,
        mesh=mesh,
        in_specs=(P("rows", "section"), P("rows"), P(), P()),
        out_specs=P("rows", "section"),
        check_vma=False,
    )
```

time: 121 us -> 34.6 us (0.29)
  the two profiles are of different devices: /device:TPU:3 before, /device:TPU:0 now
where the time goes in v1:
time: 34.6 us; the launch traced here: 34.4 us
  Pallas kernels  30.3 us (88%)
  local copies, waits for them, and re-layouts  4.16 us (12%)
    pallas_call x1, Pallas kernels, step(): pl.pallas_call(functools.partial(kernel, n), name='filter_project', out_s...  30.3 us
    unnamed x2, local copies, waits for them, and re-layouts  4.16 us

profile of v1, /device:TPU:0, one launch (start us, length us, event | category | flops | bytes accessed | tf_op | source)
XLA Modules:
  0.0 34.4 jit_solution(1689616101427028062)
XLA Ops:
  0.0 1.9 %copy.5.table_ref = f32[1024,32]{1,0:T(8,128)} copy(f32[1024,32]{0,1:T(8,128)} %param.4) | data formatting | bytes 262144 | tf_op args[0]
  1.9 30.3 %filter_project.1 = bf16[1024,512]{1,0:T(8,128)(2,1)} custom-call(f32[1024,32]{1,0:T(8,128)} %copy.5.table_ref, s32[8,128]{1,0:T(8,128)} %bitcast.2, f32[64,1024]{1,0:T(8,128)} %w_ref.1, f32[1,1024]{1,0:T(1,128)} %bitcast.3), custom_call_target="tpu_custom_call" | custom-call | tf_op jit(solution)/shard_map/filter_project/pallas_call | solution.py:183
  32.2 2.3 %copy.7 = bf16[1024,512]{1,0:T(8,128)(2,1)} copy(bf16[1024,512]{1,0:T(8,128)(2,1)} %filter_project.1) | data formatting | bytes 2097152

commit v2 on v1

v2 whole, which is shorter than its diff:
```python
import functools

import jax
import jax.numpy as jnp
from jax import lax
from jax.experimental import pallas as pl
from jax.experimental.pallas import tpu as pltpu
from jax.sharding import PartitionSpec as P

CHUNKS = 4
PLANE = 4
RAW = 4
F32 = jnp.float32
BF16 = jnp.bfloat16
I32 = jnp.int32


def split(x, terms):
    parts = []
    for _ in range(terms):
        part = x.astype(BF16)
        parts.append(part)
        x = x - part.astype(F32)
    return parts


def kernel(
    n, table_hbm, mask_hbm, w_hbm, bias_hbm, out_ref,
    table_ref, mask_ref, bias_ref,
    tally, planes, prefix, raw, hold, came, joined, w_ref, wcat,
    send_sem, recv_sem, raw_send, raw_recv, count_send, count_recv, plane_send, plane_recv, load_sem,
):
    half, height = table_hbm.shape
    width = out_ref.shape[1]
    lines = height // 128
    levels = (n - 1).bit_length()
    lanes = height // CHUNKS
    side = min(PLANE, n)
    crowd = min(RAW, n)
    first = (crowd - 1).bit_length()
    count_planes = n // side
    me = lax.axis_index("rows")
    core = lax.axis_index("section")
    plane = me // side
    seat = lax.rem(me, side)

    columns = pl.ds(pl.multiple_of(core * width, 128), width)
    mask_copy = pltpu.make_async_copy(mask_hbm, mask_ref, load_sem.at[0])
    table_copy = pltpu.make_async_copy(table_hbm, table_ref, load_sem.at[1])
    w_copy = pltpu.make_async_copy(w_hbm.at[:, columns], w_ref, load_sem.at[2])
    bias_copy = pltpu.make_async_copy(bias_hbm.at[:, columns], bias_ref, load_sem.at[3])
    for load in (mask_copy, table_copy, w_copy, bias_copy):
        load.start()

    def seat_peer(step):
        return plane * side + lax.rem(seat + step, side)

    def plane_peer(step):
        return lax.rem(plane + step, count_planes) * side + seat

    barrier = pltpu.get_barrier_semaphore()
    for step in range(1, side):
        pl.semaphore_signal(barrier, inc=1, device_id={"rows": seat_peer(step)})
    for step in range(1, count_planes):
        pl.semaphore_signal(barrier, inc=1, device_id={"rows": plane_peer(step)})
    pl.semaphore_signal(barrier, inc=1, device_id={"section": 1 - core})

    mask_copy.wait()
    mask = mask_ref[...]
    ones = mask.astype(F32).astype(BF16)
    row = lax.broadcasted_iota(I32, (128, 128), 0)
    col = lax.broadcasted_iota(I32, (128, 128), 1)
    before = jnp.where(row < col, 1.0, 0.0).astype(BF16)
    inner = jnp.dot(ones, before, preferred_element_type=F32).astype(I32)
    sums = jnp.dot(ones, jnp.ones((128, 128), BF16), preferred_element_type=F32).astype(I32)
    running = jnp.zeros((1, 128), I32)
    starts = []
    for line in range(lines):
        starts.append(running)
        running = running + sums[line : line + 1]
    tally[seat] = running
    slot = jnp.where(mask == 1, inner + jnp.concatenate(starts, 0), -1)

    own = lax.rem(me, crowd)
    table_copy.wait()
    turned = jnp.concatenate(split(table_ref[...], 3), 0)
    for chunk in range(CHUNKS):
        here = chunk * lanes + lax.broadcasted_iota(I32, (lanes, 128), 0)
        hot = jnp.concatenate(
            [jnp.where(here == slot[b : b + 1], 1.0, 0.0).astype(BF16) for b in range(lines)], 1
        )
        folded = lax.dot_general(
            turned, hot, (((1,), (1,)), ((), ())), preferred_element_type=F32
        )
        raw[own, :, chunk * lanes : (chunk + 1) * lanes] = (
            folded[:half] + folded[half : 2 * half]
        ) + folded[2 * half :]

    pl.semaphore_wait(barrier, side + count_planes - 1)

    def seat_copy(step):
        return pltpu.make_async_remote_copy(
            src_ref=tally.at[seat], dst_ref=tally.at[seat],
            send_sem=count_send.at[step], recv_sem=count_recv.at[step],
            device_id={"rows": seat_peer(step)},
        )

    def plane_copy(step):
        return pltpu.make_async_remote_copy(
            src_ref=planes.at[plane], dst_ref=planes.at[plane],
            send_sem=plane_send.at[step], recv_sem=plane_recv.at[step],
            device_id={"rows": plane_peer(step)},
        )

    def raw_copy(step):
        return pltpu.make_async_remote_copy(
            src_ref=raw.at[own], dst_ref=raw.at[own],
            send_sem=raw_send.at[step], recv_sem=raw_recv.at[step],
            device_id={"rows": me - own + lax.rem(own + step, crowd)},
        )

    for step in range(1, side):
        seat_copy(step).start()
    for step in range(1, crowd):
        raw_copy(step).start()
    for step in range(1, side):
        seat_copy(step).wait_recv()
    everyone = jnp.zeros((1, 128), I32)
    for at in range(side):
        everyone = everyone + tally[at]
    planes[plane] = everyone
    for step in range(1, count_planes):
        plane_copy(step).start()

    w_copy.wait()
    bias_copy.wait()
    bias = bias_ref[...]
    w_hi, w_lo = split(w_ref[...], 2)
    b_hi, b_mid, b_lo = [part.astype(F32) for part in split(bias, 3)]
    line = lax.broadcasted_iota(I32, (16, width), 0)
    extra = jnp.where(line == 0, b_hi, jnp.where(line == 1, b_mid, jnp.where(line == 2, b_lo, 0.0)))
    wcat[...] = jnp.concatenate([w_hi, w_lo, w_hi, extra.astype(BF16)], 0)

    for step in range(1, count_planes):
        plane_copy(step).wait_recv()
    total = jnp.zeros((1, 128), I32)
    for at in range(count_planes):
        prefix[at * side] = total
        total = total + planes[at]
    prefix[n] = total
    running = prefix[plane * side]
    for at in range(side - 1):
        running = running + tally[at]
        prefix[plane * side + at + 1] = running

    def wide(x):
        return jnp.concatenate([x] * (lanes // 128), 1)

    def data_copy(level, chunk):
        at = (slice(None), pl.ds(chunk * lanes, lanes))
        return pltpu.make_async_remote_copy(
            src_ref=hold.at[(level,) + at], dst_ref=came.at[(level,) + at],
            send_sem=send_sem.at[level, chunk], recv_sem=recv_sem.at[level, chunk],
            device_id={"rows": me + (1 - 2 * (me // (1 << level) % 2)) * (1 << level)},
        )

    def join_copy(chunk):
        at = (core, slice(None), pl.ds(chunk * lanes, lanes))
        return pltpu.make_async_remote_copy(
            src_ref=joined.at[at], dst_ref=joined.at[at],
            send_sem=send_sem.at[levels, chunk], recv_sem=recv_sem.at[levels, chunk],
            device_id={"section": 1 - core},
        )

    for step in range(1, crowd):
        raw_copy(step).wait_recv()
    turns = []
    for at in range(crowd):
        shift = (prefix[me - own + at] & (height - 1))[0, 0]
        turns.append(pltpu.roll(raw[at], shift, 1))
    low = wide(prefix[me - own])
    for chunk in range(CHUNKS):
        at = slice(chunk * lanes, (chunk + 1) * lanes)
        base = own * height + chunk * lanes + lax.broadcasted_iota(I32, (1, lanes), 1)
        place = low + ((base - low) & (crowd * height - 1))
        place = jnp.broadcast_to(place, (half, lanes))
        block = turns[0][:, at]
        for other in range(1, crowd):
            block = jnp.where(place >= wide(prefix[me - own + other]), turns[other][:, at], block)
        hold[first, :, at] = block
        data_copy(first, chunk).start()

    for level in range(first, levels):
        reach = 2 << level
        group = me // reach * reach
        bit = me // (1 << level) % 2
        low = wide(prefix[group])
        middle = wide(prefix[group + (1 << level)])
        for chunk in range(CHUNKS):
            at = slice(chunk * lanes, (chunk + 1) * lanes)
            data_copy(level, chunk).wait_recv()
            base = (me % reach) * height + chunk * lanes
            base = base + lax.broadcasted_iota(I32, (1, lanes), 1)
            place = low + ((base - low) & (reach * height - 1))
            upper = jnp.where(place >= middle, 1, 0)
            foreign = jnp.broadcast_to(upper, (half, lanes)) != bit
            block = jnp.where(foreign, came[level, :, at], hold[level, :, at])
            if level < levels - 1:
                hold[level + 1, :, at] = block
                data_copy(level + 1, chunk).start()
            else:
                joined[core, :, at] = block
                join_copy(chunk).start()

    ends = wide(total)
    for chunk in range(CHUNKS):
        at = slice(chunk * lanes, (chunk + 1) * lanes)
        join_copy(chunk).wait_recv()
        owned = me * height + chunk * lanes + lax.broadcasted_iota(I32, (1, lanes), 1)
        filled = jnp.where(owned < ends, 1.0, 0.0)
        rows = jnp.concatenate([joined[0, :, at], joined[1, :, at]], 0)
        rows = jnp.where(jnp.broadcast_to(filled, rows.shape) > 0.5, rows, 0.0)
        a_hi, a_lo = split(rows, 2)
        marks = jnp.broadcast_to(filled, (16, lanes)).astype(BF16)
        lhs = jnp.concatenate([a_hi, a_hi, a_lo, marks], 0)
        out_ref[at, :] = lax.dot_general(
            lhs, wcat[...], (((0,), (0,)), ((), ())), preferred_element_type=F32
        ).astype(BF16)

    for step in range(1, side):
        seat_copy(step).wait_send()
    for step in range(1, count_planes):
        plane_copy(step).wait_send()
    for step in range(1, crowd):
        raw_copy(step).wait_send()
    for level in range(first, levels):
        for chunk in range(CHUNKS):
            data_copy(level, chunk).wait_send()
    for chunk in range(CHUNKS):
        join_copy(chunk).wait_send()


def solution(mesh):
    n, sections = mesh.shape["rows"], mesh.shape["section"]

    def step(table, mask, weight, bias):
        height, half = table.shape
        cols, features = weight.shape
        width = features // sections
        levels = (n - 1).bit_length()
        side, crowd = min(PLANE, n), min(RAW, n)
        vmem = pl.BlockSpec(memory_space=pltpu.VMEM)
        sem = pltpu.SemaphoreType.DMA
        return pl.pallas_call(
            functools.partial(kernel, n),
            name="filter_project",
            out_shape=jax.ShapeDtypeStruct((height, width), BF16),
            in_specs=[pl.BlockSpec(memory_space=pltpu.HBM)] * 4,
            out_specs=vmem,
            scratch_shapes=[
                pltpu.VMEM((half, height), F32),
                pltpu.VMEM((height // 128, 128), I32),
                pltpu.VMEM((1, width), F32),
                pltpu.VMEM((side, 1, 128), I32),
                pltpu.VMEM((n // side, 1, 128), I32),
                pltpu.VMEM((n + 1, 1, 128), I32),
                pltpu.VMEM((crowd, half, height), F32),
                pltpu.VMEM((levels, half, height), F32),
                pltpu.VMEM((levels, half, height), F32),
                pltpu.VMEM((sections, half, height), F32),
                pltpu.VMEM((cols, width), F32),
                pltpu.VMEM((3 * cols + 16, width), BF16),
                sem((levels + 1, CHUNKS)), sem((levels + 1, CHUNKS)),
                sem((crowd,)), sem((crowd,)),
                sem((side,)), sem((side,)),
                sem((n // side,)), sem((n // side,)),
                sem((4,)),
            ],
            compiler_params=pltpu.CompilerParams(
                collective_id=0, has_side_effects=True, vmem_limit_bytes=16 << 20
            ),
        )(table.T, mask.reshape(height // 128, 128), weight, bias.reshape(1, features))

    return jax.shard_map(
        step,
        mesh=mesh,
        in_specs=(P("rows", "section"), P("rows"), P(), P()),
        out_specs=P("rows", "section"),
        check_vma=False,
    )
```

time: 34.6 us -> 28.6 us (0.83)
  Pallas kernels: 30.3 us -> 24.2 us
    pallas_call x1, Pallas kernels: 30.3 us -> 24.2 us  [step(): pl.pallas_call(functools.partial(kernel, n), name='filter_project', out_s...]
    unnamed x2 -> x9, local copies, waits for them, and re-layouts: 4.16 us -> 4.2 us
where the time goes in v2:
time: 28.6 us; the launch traced here: 28.4 us
  Pallas kernels  24.2 us (85%)
  local copies, waits for them, and re-layouts  4.2 us (15%)
    pallas_call x1, Pallas kernels, step(): pl.pallas_call(functools.partial(kernel, n), name='filter_project', out_s...  24.2 us
    unnamed x9, local copies, waits for them, and re-layouts  4.2 us

profile of v2, /device:TPU:0, one launch (start us, length us, event | category | flops | bytes accessed | tf_op | source)
XLA Modules:
  0.0 28.4 jit_solution(1053007844599006163)
XLA Ops:
  0.0 0.0 copy-start.2
  0.0 0.7 %copy-done.2 = s32[1024]{0:T(1024)S(1)} copy-done((s32[1024]{0:T(1024)S(1)}, s32[1024]{0:T(1024)}, u32[]{:S(2)}) %copy-start.2) | copy-done | bytes 4120
  0.7 0.0 copy-start
  0.7 0.9 %copy-done = f32[64,1024]{1,0:T(8,128)S(1)} copy-done((f32[64,1024]{1,0:T(8,128)S(1)}, f32[64,1024]{1,0:T(8,128)}, u32[]{:S(2)}) %copy-start) | copy-done | bytes 262168
  1.6 0.0 copy-start.1
  1.6 0.9 %copy-done.1 = f32[1024,32]{0,1:T(8,128)S(1)} copy-done((f32[1024,32]{0,1:T(8,128)S(1)}, f32[1024,32]{0,1:T(8,128)}, u32[]{:S(2)}) %copy-start.1) | copy-done | bytes 131096
  2.5 0.0 copy-start.3
  2.5 0.7 %copy-done.3 = f32[1024]{0:T(1024)S(1)} copy-done((f32[1024]{0:T(1024)S(1)}, f32[1024]{0:T(1024)}, u32[]{:S(2)}) %copy-start.3) | copy-done | bytes 4120
  3.2 24.2 %filter_project.1 = bf16[1024,512]{1,0:T(8,128)(2,1)S(1)} custom-call(f32[32,1024]{1,0:T(8,128)S(1)} %bitcast.3, s32[8,128]{1,0:T(8,128)S(1)} %bitcast.4, f32[64,1024]{1,0:T(8,128)S(1)} %copy-done, f32[1,1024]{1,0:T(1,128)S(1)} %bitcast.5), custom_call_target="tpu_custom_call" | custom-call | tf_op jit(solution)/shard_map/filter_project/pallas_call | solution.py:254
  27.4 1.0 %copy.6 = bf16[1024,512]{1,0:T(8,128)(2,1)} copy(bf16[1024,512]{1,0:T(8,128)(2,1)S(1)} %filter_project.1) | data formatting | bytes 2097152
Async XLA Ops:
  0.0 0.7 %copy-start.2 = (s32[1024]{0:T(1024)S(1)}, s32[1024]{0:T(1024)}, u32[]{:S(2)}) copy-start(s32[1024]{0:T(1024)} %param.5) | copy-start | bytes 12292
  0.7 0.9 %copy-start = (f32[64,1024]{1,0:T(8,128)S(1)}, f32[64,1024]{1,0:T(8,128)}, u32[]{:S(2)}) copy-start(f32[64,1024]{1,0:T(8,128)} %w_hbm.1) | copy-start | bytes 786436
  1.6 0.9 %copy-start.1 = (f32[1024,32]{0,1:T(8,128)S(1)}, f32[1024,32]{0,1:T(8,128)}, u32[]{:S(2)}) copy-start(f32[1024,32]{0,1:T(8,128)} %param.4) | copy-start | bytes 393220
  2.5 0.7 %copy-start.3 = (f32[1024]{0:T(1024)S(1)}, f32[1024]{0:T(1024)}, u32[]{:S(2)}) copy-start(f32[1024]{0:T(1024)} %param.7) | copy-start | bytes 12292

commit v3 on v2

--- a/solution.py
+++ b/solution.py
@@ -249,6 +249,7 @@
         width = features // sections
         levels = (n - 1).bit_length()
         side, crowd = min(PLANE, n), min(RAW, n)
+        operands = table.T, mask.reshape(height // 128, 128), weight, bias.reshape(1, features)
         vmem = pl.BlockSpec(memory_space=pltpu.VMEM)
         sem = pltpu.SemaphoreType.DMA
         return pl.pallas_call(
@@ -279,7 +280,7 @@
             compiler_params=pltpu.CompilerParams(
                 collective_id=0, has_side_effects=True, vmem_limit_bytes=16 << 20
             ),
-        )(table.T, mask.reshape(height // 128, 128), weight, bias.reshape(1, features))
+        )(*[pltpu.with_memory_space_constraint(x, pltpu.HBM) for x in operands])
 
     return jax.shard_map(
         step,

time: 28.6 us -> 25.1 us (0.88)
  local copies, waits for them, and re-layouts: 4.2 us -> 0.97 us
    unnamed x9 -> x1, local copies, waits for them, and re-layouts: 4.2 us -> 0.97 us
where the time goes in v3:
time: 25.1 us; the launch traced here: 25 us
  Pallas kernels  24 us (96%)
  local copies, waits for them, and re-layouts  0.97 us (4%)
    pallas_call x1, Pallas kernels, step(): pl.pallas_call(functools.partial(kernel, n), name='filter_project', out_s...  24 us
    unnamed x1, local copies, waits for them, and re-layouts  0.97 us

profile of v3, /device:TPU:0, one launch (start us, length us, event | category | flops | bytes accessed | tf_op | source)
XLA Modules:
  0.0 25.0 jit_solution(9402000386781761495)
XLA Ops:
  0.0 24.0 %filter_project.1 = bf16[1024,512]{1,0:T(8,128)(2,1)S(1)} custom-call(f32[32,1024]{1,0:T(8,128)} %bitcast.3, s32[8,128]{1,0:T(8,128)} %bitcast.4, f32[64,1024]{1,0:T(8,128)} %w_hbm.1, f32[1,1024]{1,0:T(1,128)} %bitcast.5), custom_call_target="tpu_custom_call" | custom-call | tf_op jit(solution)/shard_map/filter_project/pallas_call | solution.py:255
  24.0 1.0 %copy.6 = bf16[1024,512]{1,0:T(8,128)(2,1)} copy(bf16[1024,512]{1,0:T(8,128)(2,1)S(1)} %filter_project.1) | data formatting | bytes 2097152

commit v4 on v3

--- a/solution.py
+++ b/solution.py
@@ -87,10 +87,10 @@
     for chunk in range(CHUNKS):
         here = chunk * lanes + lax.broadcasted_iota(I32, (lanes, 128), 0)
         hot = jnp.concatenate(
-            [jnp.where(here == slot[b : b + 1], 1.0, 0.0).astype(BF16) for b in range(lines)], 1
+            [jnp.where(here == slot[b : b + 1], 1.0, 0.0).astype(BF16) for b in range(chunk * lanes // 128, lines)], 1
         )
         folded = lax.dot_general(
-            turned, hot, (((1,), (1,)), ((), ())), preferred_element_type=F32
+            turned[:, chunk * lanes :], hot, (((1,), (1,)), ((), ())), preferred_element_type=F32
         )
         raw[own, :, chunk * lanes : (chunk + 1) * lanes] = (
             folded[:half] + folded[half : 2 * half]

time: 25.1 us -> 25.1 us (level)
  no operation moved by 1% of the time
where the time goes in v4:
time: 25.1 us; the launch traced here: 25 us
  Pallas kernels  24 us (96%)
  local copies, waits for them, and re-layouts  0.97 us (4%)
    pallas_call x1, Pallas kernels, step(): pl.pallas_call(functools.partial(kernel, n), name='filter_project', out_s...  24 us
    unnamed x1, local copies, waits for them, and re-layouts  0.97 us

profile of v4, /device:TPU:0, one launch (start us, length us, event | category | flops | bytes accessed | tf_op | source)
XLA Modules:
  0.0 25.0 jit_solution(12064830996008831662)
XLA Ops:
  0.0 24.0 %filter_project.1 = bf16[1024,512]{1,0:T(8,128)(2,1)S(1)} custom-call(f32[32,1024]{1,0:T(8,128)} %bitcast.3, s32[8,128]{1,0:T(8,128)} %bitcast.4, f32[64,1024]{1,0:T(8,128)} %w_hbm.1, f32[1,1024]{1,0:T(1,128)} %bitcast.5), custom_call_target="tpu_custom_call" | custom-call | tf_op jit(solution)/shard_map/filter_project/pallas_call | solution.py:255
  24.0 1.0 %copy.6 = bf16[1024,512]{1,0:T(8,128)(2,1)} copy(bf16[1024,512]{1,0:T(8,128)(2,1)S(1)} %filter_project.1) | data formatting | bytes 2097152
